TPU v7x, 32 devices: a whole 2x2x4 slice. The times are simulated.
32 devices in a mesh: group: 4 (over y, x), rank: 8 (over z, core).
Axes of the slice: x: 2, y: 2, z: 4, core: 2. Of those that a mesh axis runs over, the one named last changes fastest.
Arguments:
- queries: bfloat16 [8192, 2048], P(('group', 'rank')), may hold values from -32 to 32
- key_rows: bfloat16 [8192, 2048], P(('group', 'rank')), may hold values from -6 to 6
- value_rows: bfloat16 [8192, 2048], P(('group', 'rank')), may hold values from -6 to 6
- tile_links: int32 [64, 8], P(('group', 'rank')), may hold values from 0 to 15, as said below
- link_counts: int32 [64], P(('group', 'rank')), may hold values from 1 to 8, 256 in all
Outputs:
- attended: bfloat16 [8192, 2048], P(('group', 'rank'))
Inputs may be any that keep to these rules, and one draw needn't show every extreme that they name: `tile_links`: each row names 8 different candidates.
All inputs are finite; a program needn't handle non-finite values. No bound on the sum of `link_counts` on one device may be relied on, other than what follows from the above.
Results may differ from a plain program's by a relative error of at most 0.0045.
Values may be sent and summed in bfloat16 or wider, within the bound.
A program may use at most 128 MiB of HBM per device.

v0:
```python
import jax
import jax.numpy as jnp
from jax import lax
from jax.sharding import PartitionSpec as P

H = 16
HD = 128
LMAX = 8


def passed_along(block, axis, distance):
    devices = range(lax.axis_size(axis))
    route = [((i - distance) % len(devices), i) for i in devices]
    return lax.ppermute(block, axis, route)


def shards(queries, key_rows, value_rows, tile_links, link_counts):
    rows_dev, row_width = queries.shape
    tiles_dev = tile_links.shape[0]
    tile_rows = rows_dev // tiles_dev
    groups = lax.axis_size("group")
    chains = []
    for step_by in (1, -1):
        current = (key_rows, value_rows)
        reached = []
        for repeat_index in range(2):
            current = passed_along((current[0], current[1]), "rank", step_by)
            reached.append(current)
        chains.append(reached)
    near_tiles = [chains[0][1], chains[0][0], chains[1][0], chains[1][1]]
    gathered = (
        lax.all_gather(key_rows, "group", axis=0, tiled=True),
        lax.all_gather(value_rows, "group", axis=0, tiled=True),
    )
    group_id = lax.axis_index("group")
    sources = [(key_rows, value_rows)] + list(near_tiles)
    for peer_step in range(1, groups):
        start = (group_id + peer_step) % groups * rows_dev
        sources.append(
            (
                lax.dynamic_slice_in_dim(gathered[0], start, rows_dev, 0),
                lax.dynamic_slice_in_dim(gathered[1], start, rows_dev, 0),
            )
        )
    cand_total = len(sources) * tiles_dev
    cand_ids = jnp.arange(cand_total, dtype=jnp.int32)
    listed = (tile_links[:, :, None] == cand_ids[None, None, :]) & (
        jnp.arange(LMAX, dtype=jnp.int32)[None, :, None] < link_counts[:, None, None]
    )
    own_slot = jnp.arange(tiles_dev, dtype=jnp.int32)[:, None] == cand_ids[None, :]
    multiplicity = jnp.sum(listed.astype(jnp.float32), axis=1) + own_slot.astype(jnp.float32)
    query_heads = queries.reshape(rows_dev, H, HD)
    blocks = []
    row_max = None
    for source_index, (source_keys, source_values) in enumerate(sources):
        scores = jnp.einsum(
            "qhd,khd->hqk",
            query_heads,
            source_keys.reshape(rows_dev, H, HD),
            preferred_element_type=jnp.float32,
        ) * HD ** (-0.5)
        scores = scores.reshape(H, tiles_dev, tile_rows, tiles_dev, tile_rows)
        counted = multiplicity[:, source_index * tiles_dev : (source_index + 1) * tiles_dev]
        scores = jnp.where(counted[None, :, None, :, None] > 0, scores, -jnp.inf)
        block_max = jnp.max(scores, axis=(3, 4), keepdims=True)
        row_max = block_max if row_max is None else jnp.maximum(row_max, block_max)
        blocks.append((scores, counted, source_values))
    row_total = jnp.zeros((H, tiles_dev, tile_rows), jnp.float32)
    mixed_rows = jnp.zeros((rows_dev, H, HD), jnp.float32)
    for scores, counted, source_values in blocks:
        weights = jnp.exp(scores - row_max)
        factor = counted[None, :, None, :, None]
        row_total = row_total + jnp.sum(weights * factor, axis=(3, 4))
        rounded = weights.astype(jnp.bfloat16) * factor.astype(jnp.bfloat16)
        mixed_rows = mixed_rows + jnp.einsum(
            "hqk,khd->qhd",
            rounded.reshape(H, rows_dev, rows_dev),
            source_values.reshape(rows_dev, H, HD),
            preferred_element_type=jnp.float32,
        )
    totals = jnp.transpose(row_total.reshape(H, rows_dev))
    return (mixed_rows / totals[:, :, None]).reshape(rows_dev, row_width).astype(jnp.bfloat16)


def solution(mesh):
    return jax.shard_map(
        shards,
        mesh=mesh,
        in_specs=(
            P(("group", "rank"), None),
            P(("group", "rank"), None),
            P(("group", "rank"), None),
            P(("group", "rank"), None),
            P(("group", "rank")),
        ),
        out_specs=P(("group", "rank"), None),
        check_vma=False,
    )
```

profile of v0, /device:TPU:0, one launch (start us, length us, event | category | flops | bytes accessed | tf_op | source)
XLA Modules:
  0.0 172.8 jit_solution(18075383980347148662)
XLA Ops:
  6.6 0.7 all-gather.5.cloned.1.call-update
  7.3 2.3 %copy.114 = bf16[256,2048]{0,1:T(8,128)(2,1)} copy(bf16[256,2048]{1,0:T(8,128)(2,1)} %param.6) | data formatting | bytes 2097152 | tf_op args[1]
  9.6 4.6 %collective-permute-start.2 = (bf16[256,2048]{0,1:T(8,128)(2,1)}, bf16[256,2048]{0,1:T(8,128)(2,1)}, u32[]{:S(2)}, u32[]{:S(2)}) collective-permute-start(bf16[256,2048]{0,1:T(8,128)(2,1)} %copy.114), channel_id=1, source_target_pairs={{1,0},{2,1},{3,2},{4,3},{5,4},{6,5},{7,6},{0,7},{9,8},{10,9},{11,1... | collective-permute-start | bytes 3145736 | tf_op jit(solution)/shard_map/ppermute | solution.py:14
  14.2 3.6 %collective-permute-start.6 = (bf16[256,2048]{1,0:T(8,128)(2,1)S(1)}, bf16[256,2048]{1,0:T(8,128)(2,1)}, u32[]{:S(2)}, u32[]{:S(2)}) collective-permute-start(bf16[256,2048]{1,0:T(8,128)(2,1)S(1)} %copy-done.6), channel_id=1, source_target_pairs={{1,0},{2,1},{3,2},{4,3},{5,4},{6,5},{7,6},{0,7},{9,8},{10,9},{11,1... | collective-permute-start | bytes 3145736 | tf_op jit(solution)/shard_map/ppermute | solution.py:14
  18.0 0.1 broadcast_in_dim.117
  18.2 0.2 copy.110
  18.9 0.8 copy_bitcast_fusion.3
  20.0 0.9 copy_bitcast_fusion.5
  21.2 0.8 copy_bitcast_fusion
  22.0 3.3 %fusion = (f32[16,256]{1,0:T(8,128)}, f32[16,256,256]{1,2,0:T(8,128)}) fusion(pred[256,256]{0,1:T(8,128)(4,1)S(1)} %copy.110, bf16[256,2048]{1,0:T(8,128)(2,1)S(1)} %copy-done.9, bf16[256,2048]{1,0:T(8,128)(2,1)S(1)} %copy-done), kind=kOutput, calls=%fused_computation.24 | convolution fusion | flops 271577088 | bytes 6373376 | tf_op jit(solution)/shard_map/qhd,khd->hqk/dot_general | solution.py:56
  25.4 12.7 %collective-permute-done.2 = bf16[256,2048]{0,1:T(8,128)(2,1)} collective-permute-done((bf16[256,2048]{0,1:T(8,128)(2,1)}, bf16[256,2048]{0,1:T(8,128)(2,1)}, u32[]{:S(2)}, u32[]{:S(2)}) %collective-permute-start.2) | collective-permute-done | bytes 1048608 | tf_op jit(solution)/shard_map/ppermute | solution.py:14
  38.0 3.7 %collective-permute-start.3 = (bf16[256,2048]{0,1:T(8,128)(2,1)}, bf16[256,2048]{0,1:T(8,128)(2,1)}, u32[]{:S(2)}, u32[]{:S(2)}) collective-permute-start(bf16[256,2048]{0,1:T(8,128)(2,1)} %collective-permute-done.2), channel_id=1, source_target_pairs={{1,0},{2,1},{3,2},{4,3},{5,4},{6,5},{7,6},{0,7},{9,8},{10,9},{11,1... | collective-permute-start | bytes 3145736 | tf_op jit(solution)/shard_map/ppermute | solution.py:14
  41.8 22.5 %collective-permute-done.4 = bf16[256,2048]{1,0:T(8,128)(2,1)} collective-permute-done((bf16[256,2048]{1,0:T(8,128)(2,1)S(1)}, bf16[256,2048]{1,0:T(8,128)(2,1)}, u32[]{:S(2)}, u32[]{:S(2)}) %collective-permute-start.4) | collective-permute-done | bytes 1048608 | tf_op jit(solution)/shard_map/ppermute | solution.py:14
  64.2 3.5 %collective-permute-start.7 = (bf16[256,2048]{1,0:T(8,128)(2,1)}, bf16[256,2048]{1,0:T(8,128)(2,1)}, u32[]{:S(2)}, u32[]{:S(2)}) collective-permute-start(bf16[256,2048]{1,0:T(8,128)(2,1)} %collective-permute-done.6), channel_id=1, source_target_pairs={{1,0},{2,1},{3,2},{4,3},{5,4},{6,5},{7,6},{0,7},{9,8},{10,9},{11,1... | collective-permute-start | bytes 3145736 | tf_op jit(solution)/shard_map/ppermute | solution.py:14
  67.8 1.3 copy.182
  69.4 0.2 copy.139
  69.7 0.8 copy.136
  70.7 0.8 copy.132
  72.5 0.7 copy.310
  73.4 0.7 copy.308
  74.2 0.7 copy.309
  75.0 0.1 mul.284
  75.1 0.7 copy.306
  75.9 0.1 mul.264
  76.0 0.7 copy.311
  76.8 0.1 mul.288
  77.0 0.7 copy.305
  77.7 0.1 mul.292
  77.9 0.7 copy.304
  78.7 0.7 copy.307
  79.7 0.8 copy_bitcast_fusion.2
  80.5 2.3 %copy.150 = bf16[256,2048]{0,1:T(8,128)(2,1)} copy(bf16[256,2048]{1,0:T(8,128)(2,1)} %collective-permute-done.6) | data formatting | bytes 2097152 | tf_op jit(solution)/shard_map/ppermute | solution.py:14
  82.8 2.3 %copy.148 = bf16[256,2048]{0,1:T(8,128)(2,1)} copy(bf16[256,2048]{1,0:T(8,128)(2,1)} %collective-permute-done.4) | data formatting | bytes 2097152 | tf_op jit(solution)/shard_map/ppermute | solution.py:14
  85.0 4.0 %fusion.3 = (f32[16,256]{1,0:T(8,128)S(1)}, f32[16,256,256]{2,1,0:T(8,128)}) fusion(pred[256,256]{1,0:T(8,128)(4,1)S(1)} %bitcast.305, bf16[256,16,128]{0,2,1:T(8,128)(2,1)} %bitcast.2, bf16[256,2048]{1,0:T(8,128)(2,1)S(1)} %copy-done), kind=kOutput, calls=%fused_computation.27 | convolution fusion | flops 271577088 | bytes 6373376 | tf_op jit(solution)/shard_map/qhd,khd->hqk/dot_general | solution.py:56
  89.1 2.7 %fusion.2 = (f32[16,256]{1,0:T(8,128)S(1)}, f32[16,256,256]{2,1,0:T(8,128)}) fusion(pred[256,256]{1,0:T(8,128)(4,1)S(1)} %bitcast.308, bf16[256,16,128]{0,2,1:T(8,128)(2,1)S(1)} %bitcast.282, bf16[256,2048]{1,0:T(8,128)(2,1)S(1)} %copy-done), kind=kOutput, calls=%fused_computation.26 | convolution fusion | flops 271577088 | bytes 6373376 | tf_op jit(solution)/shard_map/qhd,khd->hqk/dot_general | solution.py:56
  91.8 2.3 %copy.146 = bf16[256,2048]{0,1:T(8,128)(2,1)} copy(bf16[256,2048]{1,0:T(8,128)(2,1)} %collective-permute-done.5) | data formatting | bytes 2097152 | tf_op jit(solution)/shard_map/ppermute | solution.py:14
  94.1 8.0 %collective-permute-done.7 = bf16[256,2048]{1,0:T(8,128)(2,1)} collective-permute-done((bf16[256,2048]{1,0:T(8,128)(2,1)}, bf16[256,2048]{1,0:T(8,128)(2,1)}, u32[]{:S(2)}, u32[]{:S(2)}) %collective-permute-start.7) | collective-permute-done | bytes 1048608 | tf_op jit(solution)/shard_map/ppermute | solution.py:14
  102.1 2.3 %copy.152 = bf16[256,2048]{0,1:T(8,128)(2,1)} copy(bf16[256,2048]{1,0:T(8,128)(2,1)} %collective-permute-done.7) | data formatting | bytes 2097152 | tf_op jit(solution)/shard_map/ppermute | solution.py:14
  104.4 3.9 %fusion.4 = (f32[16,256]{1,0:T(8,128)S(1)}, f32[16,256,256]{2,1,0:T(8,128)}) fusion(pred[256,256]{1,0:T(8,128)(4,1)S(1)} %bitcast.299, bf16[256,16,128]{0,2,1:T(8,128)(2,1)} %bitcast.3, bf16[256,2048]{1,0:T(8,128)(2,1)S(1)} %copy-done), kind=kOutput, calls=%fused_computation.28 | convolution fusion | flops 271577088 | bytes 6373376 | tf_op jit(solution)/shard_map/qhd,khd->hqk/dot_general | solution.py:56
  108.3 3.4 %fusion.1 = (f32[16,256]{1,0:T(8,128)}, f32[16,256,256]{2,1,0:T(8,128)}) fusion(pred[256,256]{1,0:T(8,128)(4,1)S(1)} %bitcast.302, bf16[256,16,128]{0,2,1:T(8,128)(2,1)S(1)} %bitcast.283, bf16[256,2048]{1,0:T(8,128)(2,1)S(1)} %copy-done), kind=kOutput, calls=%fused_computation.25 | convolution fusion | flops 271577088 | bytes 6373376 | tf_op jit(solution)/shard_map/qhd,khd->hqk/dot_general | solution.py:56
  111.7 3.1 %constant_dynamic-slice_fusion.2 = (bf16[256,2048]{1,0:T(8,128)(2,1)}, bf16[256,2048]{1,0:T(8,128)(2,1)S(1)}, bf16[256,2048]{1,0:T(8,128)(2,1)S(1)}) fusion(bf16[1024,2048]{1,0:T(8,128)(2,1)} %all-gather.5.cloned.1.call-done, s32[]{:T(128)S(6)} %select_n.82, s32[]{:T(128)S(6)} %select_n.88, s32[]{:T(128)S(6)} %select_n.85), kind=kLoop, calls=%fused_computation.159 | loop fusion | bytes 6291468 | tf_op jit(solution)/shard_map/dynamic_slice | solution.py:42
  114.8 2.3 %copy.153 = bf16[256,2048]{0,1:T(8,128)(2,1)} copy(bf16[256,2048]{1,0:T(8,128)(2,1)} %get-tuple-element.13) | data formatting | bytes 2097152 | tf_op jit(solution)/shard_map/dynamic_slice | solution.py:42
  117.1 1.3 copy.156
  118.4 1.3 copy.159
  119.7 2.1 %constant_dynamic-slice_fusion.5 = (bf16[256,2048]{0,1:T(8,128)(2,1)S(1)}, bf16[256,2048]{0,1:T(8,128)(2,1)S(1)}, bf16[256,2048]{0,1:T(8,128)(2,1)S(1)}) fusion(bf16[1024,2048]{0,1:T(8,128)(2,1)} %all-gather.3.cloned.1.call-done, s32[]{:T(128)S(6)} %select_n.82, s32[]{:T(128)S(6)} %select_n.88, s32[]{:T(128)S(6)} %select_n.85), kind=kLoop, calls=%fused_computation.162 | loop fusion | bytes 6291468 | tf_op jit(solution)/shard_map/dynamic_slice | solution.py:41
  121.8 0.9 fusion.15
  122.7 0.9 fusion.14
  123.7 0.9 fusion.13
  124.8 1.1 copy-done.5
  125.9 0.3 copy-done.13
  126.2 2.7 %fusion.26 = f32[16,256,128]{1,2,0:T(8,128)} fusion(bf16[256,16,128]{0,2,1:T(8,128)(2,1)S(1)} %bitcast.287, f32[16,256,256]{2,1,0:T(8,128)S(1)} %copy-done.5, f32[16,256]{1,0:T(8,128)S(1)} %maximum_maximum_fusion, pred[256,256]{1,0:T(8,128)(4,1)S(1)} %bitcast.303, bf16[256,256]{1,0:T(8,128)(2,1)S(1)} %bitcast.332), kind=kOutput, calls=%fused_computation.47 | convolution fusion | flops 273678336 | bytes 7553024 | tf_op jit(solution)/shard_map/hqk,khd->qhd/dot_general | solution.py:75
  129.0 2.8 %fusion.20 = f32[16,256,128]{1,2,0:T(8,128)} fusion(bf16[256,16,128]{0,2,1:T(8,128)(2,1)S(1)} %bitcast.286, f32[16,256,256]{2,1,0:T(8,128)S(1)} %copy-done.3, f32[16,256]{1,0:T(8,128)S(1)} %maximum_maximum_fusion, pred[256,256]{1,0:T(8,128)(4,1)S(1)} %bitcast.306, bf16[256,256]{1,0:T(8,128)(2,1)S(1)} %bitcast.333), kind=kOutput, calls=%fused_computation.43 | convolution fusion | flops 273678336 | bytes 7553024 | tf_op jit(solution)/shard_map/hqk,khd->qhd/dot_general | solution.py:75
  131.7 0.4 copy-done.11
  132.2 2.7 %fusion.23 = f32[16,256,128]{1,2,0:T(8,128)} fusion(bf16[256,16,128]{0,2,1:T(8,128)(2,1)S(1)} %bitcast.285, f32[16,256,256]{2,1,0:T(8,128)S(1)} %copy-done.4, f32[16,256]{1,0:T(8,128)S(1)} %maximum_maximum_fusion, pred[256,256]{1,0:T(8,128)(4,1)S(1)} %bitcast.309, bf16[256,256]{1,0:T(8,128)(2,1)S(1)} %bitcast.334), kind=kOutput, calls=%fused_computation.45 | convolution fusion | flops 273678336 | bytes 7553024 | tf_op jit(solution)/shard_map/hqk,khd->qhd/dot_general | solution.py:75
  134.9 2.7 %fusion.38 = f32[16,128,256]{2,1,0:T(8,128)} fusion(bf16[256,16,128]{0,2,1:T(8,128)(2,1)S(1)} %bitcast.290, f32[16,256,256]{2,1,0:T(8,128)S(1)} %get-tuple-element.48, f32[16,256]{1,0:T(8,128)S(1)} %maximum_maximum_fusion, pred[256,256]{0,1:T(8,128)(4,1)S(1)} %copy-done.29, bf16[256,256]{0,1:T(8,128)(2,1)S(1)} %bitcast.335), kind=kOutput, calls=%fused_computation.55 | convolution fusion | flops 273678336 | bytes 7553024 | tf_op jit(solution)/shard_map/hqk,khd->qhd/dot_general | solution.py:75
  137.6 0.2 copy-done.10
  137.8 0.1 copy-done.37
  138.0 2.7 %fusion.29 = f32[16,256,128]{1,2,0:T(8,128)} fusion(bf16[256,16,128]{0,2,1:T(8,128)(2,1)S(1)} %bitcast.284, f32[16,256,256]{1,2,0:T(8,128)S(1)} %copy-done.7, f32[16,256]{1,0:T(8,128)S(1)} %maximum_maximum_fusion, pred[256,256]{0,1:T(8,128)(4,1)S(1)} %copy-done.32, bf16[256,256]{0,1:T(8,128)(2,1)S(1)} %bitcast.336), kind=kOutput, calls=%fused_computation.49 | convolution fusion | flops 276824064 | bytes 7553024 | tf_op jit(solution)/shard_map/hqk,khd->qhd/dot_general | solution.py:75
  140.7 2.6 %fusion.35 = f32[16,128,256]{2,1,0:T(8,128)} fusion(bf16[256,16,128]{0,2,1:T(8,128)(2,1)S(1)} %bitcast.289, f32[16,256,256]{2,1,0:T(8,128)S(1)} %get-tuple-element.46, f32[16,256]{1,0:T(8,128)S(1)} %maximum_maximum_fusion, pred[256,256]{0,1:T(8,128)(4,1)S(1)} %copy-done.28, bf16[256,256]{0,1:T(8,128)(2,1)S(1)} %bitcast.337), kind=kOutput, calls=%fused_computation.53 | convolution fusion | flops 273678336 | bytes 7553024 | tf_op jit(solution)/shard_map/hqk,khd->qhd/dot_general | solution.py:75
  143.3 2.7 %fusion.32 = f32[16,128,256]{2,1,0:T(8,128)} fusion(bf16[256,16,128]{0,2,1:T(8,128)(2,1)S(1)} %bitcast.288, f32[16,256,256]{2,1,0:T(8,128)S(1)} %get-tuple-element.44, f32[16,256]{1,0:T(8,128)S(1)} %maximum_maximum_fusion, pred[256,256]{0,1:T(8,128)(4,1)S(1)} %copy-done.27, bf16[256,256]{0,1:T(8,128)(2,1)S(1)} %bitcast.338), kind=kOutput, calls=%fused_computation.51 | convolution fusion | flops 273678336 | bytes 7553024 | tf_op jit(solution)/shard_map/hqk,khd->qhd/dot_general | solution.py:75
  146.0 6.0 %multiply_reduce_fusion.7 = (f32[16,256]{1,0:T(8,128)S(1)}, f32[16,256]{1,0:T(8,128)S(1)}, f32[16,256]{1,0:T(8,128)}, f32[16,256]{1,0:T(8,128)}) fusion(f32[16,256,256]{1,2,0:T(8,128)S(1)} %copy-done.7, f32[256,256]{0,1:T(8,128)} %get-tuple-element.62, f32[16,256]{1,0:T(8,128)S(1)} %maximum_maximum_fusion, pred[256,256]{0,1:T(8,128)(4,1)} %copy-done.31, ...), kind=kLoop, calls=%fused_computation.10 | loop fusion | flops 20955136 | bytes 18169856 | tf_op jit(solution)/shard_map/reduce_sum | solution.py:73
  152.1 5.9 %multiply_reduce_fusion.6 = (f32[16,256]{1,0:T(8,128)S(1)}, f32[16,256]{1,0:T(8,128)S(1)}, f32[16,256]{1,0:T(8,128)S(1)}, f32[16,256]{1,0:T(8,128)S(1)}) fusion(f32[16,256,256]{2,1,0:T(8,128)S(1)} %copy-done.5, f32[16,256]{1,0:T(8,128)S(1)} %maximum_maximum_fusion, f32[256,256]{1,0:T(8,128)S(1)} %copy-done.20, pred[256,256]{1,0:T(8,128)(4,1)} %bitcast.304, ...), kind=kLoop, calls=%fused_computation.9 | loop fusion | flops 20955136 | bytes 18169856 | tf_op jit(solution)/shard_map/reduce_sum | solution.py:73
  158.1 6.4 %fusion.50 = bf16[256,16,128]{0,2,1:T(8,128)(2,1)S(1)} fusion(f32[16,128,256]{2,1,0:T(8,128)} %fusion.32, f32[16,128,256]{2,1,0:T(8,128)} %fusion.35, f32[16,128,256]{2,1,0:T(8,128)} %fusion.38, f32[16,256,128]{1,2,0:T(8,128)} %fusion.20, f32[16,256,128]{1,2,0:T(8,128)} %fusion.23, f32[16,256,128]{1,2,0:T(8,128)} %fusion.29, f32[16,256,128]{1,2,0:T(8,128)} %fusion.26, ...), kind=kOutput, calls=%fused_computation.67 | convolution fusion | flops 278396928 | bytes 21200896 | tf_op jit(solution)/shard_map/hqk,khd->qhd/dot_general | solution.py:75
  164.5 1.4 copy.166
  (144 shorter events, 4.4 us)
Async XLA Ops:
  6.5 15.5 %copy-start = (bf16[256,2048]{1,0:T(8,128)(2,1)S(1)}, bf16[256,2048]{1,0:T(8,128)(2,1)}, u32[]{:S(2)}) copy-start(bf16[256,2048]{1,0:T(8,128)(2,1)} %param.5) | copy-start | bytes 3145732
  6.5 7.7 %copy-start.6 = (bf16[256,2048]{1,0:T(8,128)(2,1)S(1)}, bf16[256,2048]{1,0:T(8,128)(2,1)}, u32[]{:S(2)}) copy-start(bf16[256,2048]{1,0:T(8,128)(2,1)} %param.7) | copy-start | bytes 3145732
  6.5 11.2 %copy-start.45 = (s32[2]{0:T(128)S(1)}, s32[2]{0:T(128)}, u32[]{:S(2)}) copy-start(s32[2]{0:T(128)} %param.9) | copy-start | bytes 28
  6.5 11.3 %copy-start.44 = (s32[2,8]{1,0:T(2,128)S(1)}, s32[2,8]{1,0:T(2,128)}, u32[]{:S(2)}) copy-start(s32[2,8]{1,0:T(2,128)} %param.8) | copy-start | bytes 196
  6.5 105.1 %all-gather.5.cloned.1.call-start = ((), (), s32[]{:S(2)}) async-start(), calls=%async_computation.1 | async-start | bytes 5242880 | tf_op jit(solution)/shard_map/all_gather | solution.py:33
  7.3 112.4 %all-gather.3.cloned.1.call-start = ((), (), s32[]{:S(2)}) async-start(), calls=%async_computation | async-start | bytes 5242880 | tf_op jit(solution)/shard_map/all_gather | solution.py:32
  9.6 28.4 %collective-permute-start.2 = (bf16[256,2048]{0,1:T(8,128)(2,1)}, bf16[256,2048]{0,1:T(8,128)(2,1)}, u32[]{:S(2)}, u32[]{:S(2)}) collective-permute-start(bf16[256,2048]{0,1:T(8,128)(2,1)} %copy.114), channel_id=1, source_target_pairs={{1,0},{2,1},{3,2},{4,3},{5,4},{6,5},{7,6},{0,7},{9,8},{10,9},{11,1... | collective-permute-start | bytes 3145736 | tf_op jit(solution)/shard_map/ppermute | solution.py:14
  14.2 70.8 %collective-permute-start = (bf16[256,2048]{0,1:T(8,128)(2,1)}, bf16[256,2048]{0,1:T(8,128)(2,1)S(1)}, u32[]{:S(2)}, u32[]{:S(2)}) collective-permute-start(bf16[256,2048]{0,1:T(8,128)(2,1)} %copy.114), channel_id=1, source_target_pairs={{7,0},{0,1},{1,2},{2,3},{3,4},{4,5},{5,6},{6,7},{15,8},{8,9},{9,10... | collective-permute-start | bytes 3145736 | tf_op jit(solution)/shard_map/ppermute | solution.py:14
  14.2 50.0 %collective-permute-start.4 = (bf16[256,2048]{1,0:T(8,128)(2,1)S(1)}, bf16[256,2048]{1,0:T(8,128)(2,1)}, u32[]{:S(2)}, u32[]{:S(2)}) collective-permute-start(bf16[256,2048]{1,0:T(8,128)(2,1)S(1)} %copy-done.6), channel_id=1, source_target_pairs={{7,0},{0,1},{1,2},{2,3},{3,4},{4,5},{5,6},{6,7},{15,8},{8,9},{9,10... | collective-permute-start | bytes 3145736 | tf_op jit(solution)/shard_map/ppermute | solution.py:14
  14.2 50.0 %collective-permute-start.6 = (bf16[256,2048]{1,0:T(8,128)(2,1)S(1)}, bf16[256,2048]{1,0:T(8,128)(2,1)}, u32[]{:S(2)}, u32[]{:S(2)}) collective-permute-start(bf16[256,2048]{1,0:T(8,128)(2,1)S(1)} %copy-done.6), channel_id=1, source_target_pairs={{1,0},{2,1},{3,2},{4,3},{5,4},{6,5},{7,6},{0,7},{9,8},{10,9},{11,1... | collective-permute-start | bytes 3145736 | tf_op jit(solution)/shard_map/ppermute | solution.py:14
  18.4 7.0 %copy-start.31 = (pred[256,256]{0,1:T(8,128)(4,1)}, pred[256,256]{0,1:T(8,128)(4,1)S(1)}, u32[]{:S(2)}) copy-start(pred[256,256]{0,1:T(8,128)(4,1)S(1)} %copy.110) | copy-start | bytes 196612
  18.6 3.4 %copy-start.9 = (bf16[256,2048]{1,0:T(8,128)(2,1)S(1)}, bf16[256,2048]{1,0:T(8,128)(2,1)}, u32[]{:S(2)}) copy-start(bf16[256,2048]{1,0:T(8,128)(2,1)} %param.6) | copy-start | bytes 3145732
  38.0 66.3 %collective-permute-start.3 = (bf16[256,2048]{0,1:T(8,128)(2,1)}, bf16[256,2048]{0,1:T(8,128)(2,1)}, u32[]{:S(2)}, u32[]{:S(2)}) collective-permute-start(bf16[256,2048]{0,1:T(8,128)(2,1)} %collective-permute-done.2), channel_id=1, source_target_pairs={{1,0},{2,1},{3,2},{4,3},{5,4},{6,5},{7,6},{0,7},{9,8},{10,9},{11,1... | collective-permute-start | bytes 3145736 | tf_op jit(solution)/shard_map/ppermute | solution.py:14
  64.2 27.6 %collective-permute-start.5 = (bf16[256,2048]{1,0:T(8,128)(2,1)}, bf16[256,2048]{1,0:T(8,128)(2,1)}, u32[]{:S(2)}, u32[]{:S(2)}) collective-permute-start(bf16[256,2048]{1,0:T(8,128)(2,1)} %collective-permute-done.4), channel_id=1, source_target_pairs={{7,0},{0,1},{1,2},{2,3},{3,4},{4,5},{5,6},{6,7},{15,8},{8,9},{9,10... | collective-permute-start | bytes 3145736 | tf_op jit(solution)/shard_map/ppermute | solution.py:14
  64.2 37.9 %collective-permute-start.7 = (bf16[256,2048]{1,0:T(8,128)(2,1)}, bf16[256,2048]{1,0:T(8,128)(2,1)}, u32[]{:S(2)}, u32[]{:S(2)}) collective-permute-start(bf16[256,2048]{1,0:T(8,128)(2,1)} %collective-permute-done.6), channel_id=1, source_target_pairs={{1,0},{2,1},{3,2},{4,3},{5,4},{6,5},{7,6},{0,7},{9,8},{10,9},{11,1... | collective-permute-start | bytes 3145736 | tf_op jit(solution)/shard_map/ppermute | solution.py:14
  69.5 52.3 %copy-start.26 = (pred[256,256]{0,1:T(8,128)(4,1)}, pred[256,256]{0,1:T(8,128)(4,1)S(1)}, u32[]{:S(2)}) copy-start(pred[256,256]{0,1:T(8,128)(4,1)S(1)} %copy.139) | copy-start | bytes 196612
  71.8 53.0 %copy-start.23 = (pred[32,8,2,128]{3,1,2,0:T(8,128)(4,1)}, pred[32,8,2,128]{3,1,2,0:T(8,128)(4,1)S(1)}, u32[]{:S(2)}) copy-start(pred[32,8,2,128]{3,1,2,0:T(8,128)(4,1)S(1)} %copy.302) | copy-start | bytes 196612
  72.0 56.9 %copy-start.24 = (pred[32,8,2,128]{3,1,2,0:T(8,128)(4,1)}, pred[32,8,2,128]{3,1,2,0:T(8,128)(4,1)S(1)}, u32[]{:S(2)}) copy-start(pred[32,8,2,128]{3,1,2,0:T(8,128)(4,1)S(1)} %copy.300) | copy-start | bytes 196612
  72.2 59.5 %copy-start.25 = (pred[32,8,2,128]{3,1,2,0:T(8,128)(4,1)}, pred[32,8,2,128]{3,1,2,0:T(8,128)(4,1)S(1)}, u32[]{:S(2)}) copy-start(pred[32,8,2,128]{3,1,2,0:T(8,128)(4,1)S(1)} %copy.301) | copy-start | bytes 196612
  85.0 23.3 %collective-permute-start.1 = (bf16[256,2048]{0,1:T(8,128)(2,1)S(1)}, bf16[256,2048]{0,1:T(8,128)(2,1)S(1)}, u32[]{:S(2)}, u32[]{:S(2)}) collective-permute-start(bf16[256,2048]{0,1:T(8,128)(2,1)S(1)} %collective-permute-done), channel_id=1, source_target_pairs={{7,0},{0,1},{1,2},{2,3},{3,4},{4,5},{5,6},{6,7},{15,8},{8,9},{9,10... | collective-permute-start | bytes 3145736 | tf_op jit(solution)/shard_map/ppermute | solution.py:14
  121.8 1.0 copy-start.28
  122.7 1.0 copy-start.29
  123.7 1.0 copy-start.40
  123.7 1.0 copy-start.43
  123.7 2.2 %copy-start.5 = (f32[16,256,256]{2,1,0:T(8,128)S(1)}, f32[16,256,256]{2,1,0:T(8,128)}, u32[]{:S(2)}) copy-start(f32[16,256,256]{2,1,0:T(8,128)} %get-tuple-element.58) | copy-start | bytes 12582916
  123.7 2.5 %copy-start.13 = (bf16[256,2048]{0,1:T(8,128)(2,1)S(1)}, bf16[256,2048]{0,1:T(8,128)(2,1)}, u32[]{:S(2)}) copy-start(bf16[256,2048]{0,1:T(8,128)(2,1)} %copy.146) | copy-start | bytes 3145732
  123.7 2.5 %copy-start.33 = (bf16[32,8,2,128]{3,1,2,0:T(8,128)(2,1)S(1)}, bf16[32,8,2,128]{3,1,2,0:T(8,128)(2,1)}, u32[]{:S(2)}) copy-start(bf16[32,8,2,128]{3,1,2,0:T(8,128)(2,1)} %copy.310) | copy-start | bytes 393220
  124.7 4.2 %copy-start.3 = (f32[16,256,256]{2,1,0:T(8,128)S(1)}, f32[16,256,256]{2,1,0:T(8,128)}, u32[]{:S(2)}) copy-start(f32[16,256,256]{2,1,0:T(8,128)} %get-tuple-element.52) | copy-start | bytes 12582916
  124.7 4.2 %copy-start.12 = (bf16[256,2048]{0,1:T(8,128)(2,1)S(1)}, bf16[256,2048]{0,1:T(8,128)(2,1)}, u32[]{:S(2)}) copy-start(bf16[256,2048]{0,1:T(8,128)(2,1)} %copy.150) | copy-start | bytes 3145732
  124.8 4.2 %copy-start.34 = (bf16[32,8,2,128]{3,1,2,0:T(8,128)(2,1)S(1)}, bf16[32,8,2,128]{3,1,2,0:T(8,128)(2,1)}, u32[]{:S(2)}) copy-start(bf16[32,8,2,128]{3,1,2,0:T(8,128)(2,1)} %copy.308) | copy-start | bytes 393220
  128.9 2.8 %copy-start.4 = (f32[16,256,256]{2,1,0:T(8,128)S(1)}, f32[16,256,256]{2,1,0:T(8,128)}, u32[]{:S(2)}) copy-start(f32[16,256,256]{2,1,0:T(8,128)} %get-tuple-element.54) | copy-start | bytes 12582916
  128.9 3.2 %copy-start.11 = (bf16[256,2048]{0,1:T(8,128)(2,1)S(1)}, bf16[256,2048]{0,1:T(8,128)(2,1)}, u32[]{:S(2)}) copy-start(bf16[256,2048]{0,1:T(8,128)(2,1)} %copy.148) | copy-start | bytes 3145732
  128.9 3.2 %copy-start.35 = (bf16[32,8,2,128]{3,1,2,0:T(8,128)(2,1)S(1)}, bf16[32,8,2,128]{3,1,2,0:T(8,128)(2,1)}, u32[]{:S(2)}) copy-start(bf16[32,8,2,128]{3,1,2,0:T(8,128)(2,1)} %copy.309) | copy-start | bytes 393220
  131.7 3.2 %copy-start.16 = (bf16[256,2048]{0,1:T(8,128)(2,1)S(1)}, bf16[256,2048]{0,1:T(8,128)(2,1)}, u32[]{:S(2)}) copy-start(bf16[256,2048]{0,1:T(8,128)(2,1)} %copy.153) | copy-start | bytes 3145732
  131.7 3.2 %copy-start.36 = (bf16[32,8,2,128]{3,1,2,0:T(8,128)(2,1)S(1)}, bf16[32,8,2,128]{3,1,2,0:T(8,128)(2,1)}, u32[]{:S(2)}) copy-start(bf16[32,8,2,128]{3,1,2,0:T(8,128)(2,1)} %copy.306) | copy-start | bytes 393220
  134.9 2.7 %copy-start.7 = (f32[16,256,256]{1,2,0:T(8,128)S(1)}, f32[16,256,256]{1,2,0:T(8,128)}, u32[]{:S(2)}) copy-start(f32[16,256,256]{1,2,0:T(8,128)} %get-tuple-element.56) | copy-start | bytes 12582916
  134.9 2.9 %copy-start.10 = (bf16[256,2048]{0,1:T(8,128)(2,1)S(1)}, bf16[256,2048]{0,1:T(8,128)(2,1)}, u32[]{:S(2)}) copy-start(bf16[256,2048]{0,1:T(8,128)(2,1)} %copy.182) | copy-start | bytes 3145732
  134.9 2.9 %copy-start.32 = (pred[256,256]{0,1:T(8,128)(4,1)S(1)}, pred[256,256]{0,1:T(8,128)(4,1)}, u32[]{:S(2)}) copy-start(pred[256,256]{0,1:T(8,128)(4,1)} %copy-done.31) | copy-start | bytes 196612
  134.9 3.1 %copy-start.37 = (bf16[32,8,2,128]{3,1,2,0:T(8,128)(2,1)S(1)}, bf16[32,8,2,128]{3,1,2,0:T(8,128)(2,1)}, u32[]{:S(2)}) copy-start(bf16[32,8,2,128]{3,1,2,0:T(8,128)(2,1)} %copy.311) | copy-start | bytes 393220
  137.6 3.0 %copy-start.15 = (bf16[256,2048]{0,1:T(8,128)(2,1)S(1)}, bf16[256,2048]{0,1:T(8,128)(2,1)}, u32[]{:S(2)}) copy-start(bf16[256,2048]{0,1:T(8,128)(2,1)} %copy.156) | copy-start | bytes 3145732
  137.6 3.1 %copy-start.38 = (bf16[32,8,2,128]{3,1,2,0:T(8,128)(2,1)S(1)}, bf16[32,8,2,128]{3,1,2,0:T(8,128)(2,1)}, u32[]{:S(2)}) copy-start(bf16[32,8,2,128]{3,1,2,0:T(8,128)(2,1)} %copy.305) | copy-start | bytes 393220
  140.6 2.7 %copy-start.14 = (bf16[256,2048]{0,1:T(8,128)(2,1)S(1)}, bf16[256,2048]{0,1:T(8,128)(2,1)}, u32[]{:S(2)}) copy-start(bf16[256,2048]{0,1:T(8,128)(2,1)} %copy.159) | copy-start | bytes 3145732
  140.6 2.7 %copy-start.27 = (pred[256,256]{0,1:T(8,128)(4,1)S(1)}, pred[256,256]{0,1:T(8,128)(4,1)}, u32[]{:S(2)}) copy-start(pred[256,256]{0,1:T(8,128)(4,1)} %copy-done.26) | copy-start | bytes 196612
  140.6 2.7 %copy-start.39 = (bf16[32,8,2,128]{3,1,2,0:T(8,128)(2,1)S(1)}, bf16[32,8,2,128]{3,1,2,0:T(8,128)(2,1)}, u32[]{:S(2)}) copy-start(bf16[32,8,2,128]{3,1,2,0:T(8,128)(2,1)} %copy.304) | copy-start | bytes 393220
  143.3 2.7 %copy-start.21 = (f32[256,256]{0,1:T(8,128)S(1)}, f32[256,256]{0,1:T(8,128)}, u32[]{:S(2)}) copy-start(f32[256,256]{0,1:T(8,128)} %get-tuple-element.59) | copy-start | bytes 786436
  143.3 2.7 %copy-start.22 = (f32[256,256]{0,1:T(8,128)S(1)}, f32[256,256]{0,1:T(8,128)}, u32[]{:S(2)}) copy-start(f32[256,256]{0,1:T(8,128)} %get-tuple-element.60) | copy-start | bytes 786436
  146.0 6.1 %copy-start.2 = (f32[16,256,256]{2,1,0:T(8,128)S(1)}, f32[16,256,256]{2,1,0:T(8,128)}, u32[]{:S(2)}) copy-start(f32[16,256,256]{2,1,0:T(8,128)} %get-tuple-element.50) | copy-start | bytes 12582916
  146.0 6.1 %copy-start.17 = (f32[256,256]{1,0:T(8,128)S(1)}, f32[256,256]{1,0:T(8,128)}, u32[]{:S(2)}) copy-start(f32[256,256]{1,0:T(8,128)} %get-tuple-element.63) | copy-start | bytes 786436
  146.0 6.1 %copy-start.18 = (f32[256,256]{1,0:T(8,128)S(1)}, f32[256,256]{1,0:T(8,128)}, u32[]{:S(2)}) copy-start(f32[256,256]{1,0:T(8,128)} %get-tuple-element.64) | copy-start | bytes 786436
  146.0 6.1 %copy-start.19 = (f32[256,256]{1,0:T(8,128)S(1)}, f32[256,256]{1,0:T(8,128)}, u32[]{:S(2)}) copy-start(f32[256,256]{1,0:T(8,128)} %get-tuple-element.65) | copy-start | bytes 786436
  146.0 6.1 %copy-start.20 = (f32[256,256]{1,0:T(8,128)S(1)}, f32[256,256]{1,0:T(8,128)}, u32[]{:S(2)}) copy-start(f32[256,256]{1,0:T(8,128)} %get-tuple-element.66) | copy-start | bytes 786436
  152.1 6.0 %copy-start.41 = (f32[16,256]{1,0:T(8,128)S(1)}, f32[16,256]{1,0:T(8,128)}, u32[]{:S(2)}) copy-start(f32[16,256]{1,0:T(8,128)} %get-tuple-element.11) | copy-start | bytes 49156
  152.1 6.0 %copy-start.42 = (f32[16,256]{1,0:T(8,128)S(1)}, f32[16,256]{1,0:T(8,128)}, u32[]{:S(2)}) copy-start(f32[16,256]{1,0:T(8,128)} %get-tuple-element.12) | copy-start | bytes 49156
  152.1 6.0 %copy-start.8 = (bf16[256,2048]{0,1:T(8,128)(2,1)S(1)}, bf16[256,2048]{0,1:T(8,128)(2,1)}, u32[]{:S(2)}) copy-start(bf16[256,2048]{0,1:T(8,128)(2,1)} %copy.152) | copy-start | bytes 3145732
  152.1 6.0 %copy-start.30 = (bf16[32,8,2,128]{3,1,2,0:T(8,128)(2,1)S(1)}, bf16[32,8,2,128]{3,1,2,0:T(8,128)(2,1)}, u32[]{:S(2)}) copy-start(bf16[32,8,2,128]{3,1,2,0:T(8,128)(2,1)} %copy.307) | copy-start | bytes 393220
  158.1 7.8 %copy-start.1 = (bf16[256,2048]{1,0:T(8,128)(2,1)S(1)}, bf16[256,2048]{1,0:T(8,128)(2,1)}, u32[]{:S(2)}) copy-start(bf16[256,2048]{1,0:T(8,128)(2,1)} %param.5) | copy-start | bytes 3145732
Sparse Core Ops, SparseCore 0:
  9.2 55.2 all-gather.4
  66.3 52.4 all-gather.2
where the time goes:
time: 173 us
  matrix products  45.4 us (26%)
  waiting for transfers between devices  43.9 us (25%)
  local copies, waits for them, and re-layouts  41.7 us (24%)
  starting transfers between devices  15.5 us (9%)
  between operations  14.1 us (8%)
  other arithmetic  12.3 us (7%)
    ppermute x8, waiting for transfers between devices, passed_along(): return lax.ppermute(block, axis, route)  43.2 us
    dot_general x8, matrix products, shards(): jnp.einsum('hqk,khd->qhd', rounded.reshape(H, rows_dev, rows_dev), source...  25.2 us
    dot_general x8, matrix products, shards(): jnp.einsum('qhd,khd->hqk', query_heads, source_keys.reshape(rows_dev, H,...  20.2 us
    ppermute x8, starting transfers between devices, passed_along(): return lax.ppermute(block, axis, route)  15.4 us
    reduce_sum x2, other arithmetic, shards(): row_total = row_total + jnp.sum(weights * factor, axis=(3, 4))  12 us
    unnamed x109, local copies, waits for them, and re-layouts  10.3 us
    ppermute x4, local copies, waits for them, and re-layouts, passed_along(): return lax.ppermute(block, axis, route)  9.07 us
    dynamic_slice x4, local copies, waits for them, and re-layouts, shards(): lax.dynamic_slice_in_dim(gathered[1], start, rows_dev, 0)  7.98 us
  transfers between devices with their start and end apart: 10, of which 3 were waited for; matrix products, arithmetic and copies ran while one was open for 31% of the time, Pallas kernels for 0%

commit v1 on v0

v1 whole, which is shorter than its diff:
```python
import functools
import math

import jax
import jax.numpy as jnp
from jax import lax
from jax.experimental import pallas as pl
from jax.experimental.pallas import tpu as pltpu
from jax.sharding import PartitionSpec as P

HD = 128
HEADS_PER_CHUNK = 2
WINDOW = 3
MESH = pl.DeviceIdType.MESH


def kernel(
    groups,
    ranks,
    q_hbm,
    k_hbm,
    v_hbm,
    links,
    counts,
    o_ref,
    land,
    q_v,
    bias,
    send_sems,
    recv_sems,
    q_sem,
):
    chunks, _, slots, rows, width = land.shape
    tiles, lmax = links.shape
    tile_rows = rows // tiles
    g = lax.axis_index("group")
    r = lax.axis_index("rank")
    core = lax.rem(r, 2)
    partner = (g, r + 1 - 2 * core)
    ahead = (g, lax.rem(r + 2, ranks))
    behind = (g, lax.rem(r + ranks - 2, ranks))
    flows = [(ahead, 1), (behind, 4)]
    for step in range(1, groups):
        flows.append(((lax.rem(g + groups - step, groups), r), 4 + step))
    flows.append((partner, 2 + core))
    relay = len(flows)

    barrier = pltpu.get_barrier_semaphore()
    for device, _ in flows:
        pl.semaphore_signal(barrier, inc=1, device_id=device, device_id_type=MESH)

    def columns(c):
        return pl.ds(pl.multiple_of(c * width, width), width)

    def own_copy(c, kv):
        src = (k_hbm, v_hbm)[kv]
        return pltpu.make_async_copy(
            src.at[:, columns(c)], land.at[c, kv, 0], recv_sems.at[c, kv, 0]
        )

    def flow_copy(c, kv, f):
        device, slot = flows[f]
        src = (k_hbm, v_hbm)[kv]
        return pltpu.make_async_remote_copy(
            src_ref=src.at[:, columns(c)],
            dst_ref=land.at[c, kv, slot],
            send_sem=send_sems.at[c, kv, f],
            recv_sem=recv_sems.at[c, kv, slot],
            device_id=device,
            device_id_type=MESH,
        )

    def relay_copy(c, kv):
        return pltpu.make_async_remote_copy(
            src_ref=land.at[c, kv, 4 - 3 * core],
            dst_ref=land.at[c, kv, 3 - core],
            send_sem=send_sems.at[c, kv, relay],
            recv_sem=recv_sems.at[c, kv, 3 - core],
            device_id=partner,
            device_id_type=MESH,
        )

    def arrived(c, kv, slot):
        pltpu.make_async_remote_copy(
            src_ref=land.at[c, kv, slot],
            dst_ref=land.at[c, kv, slot],
            send_sem=send_sems.at[c, kv, 0],
            recv_sem=recv_sems.at[c, kv, slot],
            device_id=partner,
            device_id_type=MESH,
        ).wait_recv()

    def issue(c):
        for kv in range(2):
            for f in range(len(flows)):
                flow_copy(c, kv, f).start()

    q_copy = pltpu.make_async_copy(q_hbm, q_v, q_sem)
    q_copy.start()
    pl.semaphore_wait(barrier, len(flows))

    @pl.loop(0, min(WINDOW, chunks))
    def _(c):
        issue(c)

    @pl.loop(0, chunks)
    def _(c):
        for kv in range(2):
            own_copy(c, kv).start()

    cand = lax.broadcasted_iota(jnp.int32, (1, slots * rows), 1) // tile_rows
    for i in range(tiles):
        used = jnp.where(cand == i, 1, 0)
        for j in range(lmax):
            hit = jnp.where(j < counts[i], links[i, j], -1)
            used = used + jnp.where(cand == hit, 1, 0)
        bias[i, :, :] = jnp.where(used == 0, -jnp.inf, jnp.where(used == 2, 1.0, 0.0))
    q_copy.wait()

    scale = HD ** (-0.5) * math.log2(math.e)

    def attend(c):
        for h in range(width // HD):
            cols = slice(h * HD, (h + 1) * HD)
            keys = land[c, 0, :, :, cols].reshape(slots * rows, HD)
            values = land[c, 1, :, :, cols].reshape(slots * rows, HD)
            head = pl.ds(pl.multiple_of(c * width + h * HD, HD), HD)
            scores = lax.dot_general(
                q_v[:, head], keys, (((1,), (1,)), ((), ())), preferred_element_type=jnp.float32
            )
            scores = scores.reshape(tiles, tile_rows, slots * rows) * scale + bias[...]
            scores = scores.reshape(rows, slots * rows)
            weights = jnp.exp2(scores - jnp.max(scores, axis=1, keepdims=True))
            total = jnp.sum(weights, axis=1, keepdims=True)
            mixed = jnp.dot(
                weights.astype(jnp.bfloat16), values, preferred_element_type=jnp.float32
            )
            o_ref[:, head] = (mixed / total).astype(jnp.bfloat16)

    @pl.loop(0, chunks + 1)
    def _(c):
        @pl.when(c < chunks)
        def _():
            for kv in range(2):
                arrived(c, kv, 4 - 3 * core)
                relay_copy(c, kv).start()

        @pl.when(c + WINDOW < chunks)
        def _():
            issue(c + WINDOW)

        @pl.when(c >= 1)
        def _():
            b = c - 1
            for kv in range(2):
                own_copy(b, kv).wait()
                arrived(b, kv, 1 + 3 * core)
                for slot in (2, 3) + tuple(range(5, slots)):
                    arrived(b, kv, slot)
            attend(b)

    @pl.loop(0, chunks)
    def _(c):
        for kv in range(2):
            for f in range(len(flows)):
                flow_copy(c, kv, f).wait_send()
            relay_copy(c, kv).wait_send()


def shards(groups, ranks, queries, key_rows, value_rows, tile_links, link_counts):
    rows, features = queries.shape
    tiles = tile_links.shape[0]
    slots = 4 + groups
    width = HEADS_PER_CHUNK * HD
    chunks = features // width
    hbm = pl.BlockSpec(memory_space=pl.ANY)
    smem = pl.BlockSpec(memory_space=pltpu.SMEM)
    return pl.pallas_call(
        functools.partial(kernel, groups, ranks),
        out_shape=jax.ShapeDtypeStruct((rows, features), jnp.bfloat16),
        in_specs=[hbm, hbm, hbm, smem, smem],
        out_specs=pl.BlockSpec(memory_space=pltpu.VMEM),
        scratch_shapes=[
            pltpu.VMEM((chunks, 2, slots, rows, width), jnp.bfloat16),
            pltpu.VMEM((rows, features), jnp.bfloat16),
            pltpu.VMEM((tiles, 1, slots * rows), jnp.float32),
            pltpu.SemaphoreType.DMA((chunks, 2, groups + 3)),
            pltpu.SemaphoreType.DMA((chunks, 2, slots + 1)),
            pltpu.SemaphoreType.DMA,
        ],
        compiler_params=pltpu.CompilerParams(
            collective_id=0, has_side_effects=True, vmem_limit_bytes=48 * 2**20
        ),
    )(queries, key_rows, value_rows, tile_links, link_counts)


def solution(mesh):
    nodes = P(("group", "rank"), None)
    return jax.shard_map(
        functools.partial(shards, mesh.shape["group"], mesh.shape["rank"]),
        mesh=mesh,
        in_specs=(nodes, nodes, nodes, nodes, P(("group", "rank"))),
        out_specs=nodes,
        check_vma=False,
    )
```

time: 173 us -> 109 us (0.63)
  Pallas kernels: 0 us -> 103 us
  matrix products: 45.4 us -> 0 us
  waiting for transfers between devices: 43.9 us -> 0 us
  local copies, waits for them, and re-layouts: 41.7 us -> 5.98 us
  starting transfers between devices: 15.5 us -> 0 us
  between operations: 14.1 us -> 0.01 us
  other arithmetic: 12.3 us -> 0 us
    pallas_call x0 -> x1, Pallas kernels: none -> 103 us  [shards(): pl.pallas_call(functools.partial(kernel, groups, ranks), out_shape=jax.Sh...]
    dot_general x16 -> x0, matrix products: 45.4 us -> none  [the longest x8 25.2 us: shards(): jnp.einsum('hqk,khd->qhd', rounded.reshape(H, rows_dev, rows_dev), source...]
    ppermute x8 -> x0, waiting for transfers between devices: 43.2 us -> none  [passed_along(): return lax.ppermute(block, axis, route)]
    ppermute x8 -> x0, starting transfers between devices: 15.4 us -> none  [passed_along(): return lax.ppermute(block, axis, route)]
    reduce_sum x3 -> x0, other arithmetic: 12.1 us -> none  [the longest x2 12 us: shards(): row_total = row_total + jnp.sum(weights * factor, axis=(3, 4))]
    dynamic_slice x5 -> x0, local copies, waits for them, and re-layouts: 10.1 us -> none  [the longest x4 7.98 us: shards(): lax.dynamic_slice_in_dim(gathered[1], start, rows_dev, 0)]
    ppermute x4 -> x0, local copies, waits for them, and re-layouts: 9.07 us -> none  [passed_along(): return lax.ppermute(block, axis, route)]
    mul x20 -> x0, local copies, waits for them, and re-layouts: 5.56 us -> none  [the longest x12 4.45 us: shards(): row_total = row_total + jnp.sum(weights * factor, axis=(3, 4))]
  transfers between devices with their start and end apart: 10 -> 0, of which waited for: 3 -> 0; matrix products, arithmetic and copies ran while one was open for 31% -> 0% of each run, Pallas kernels for 0% -> 0%
where the time goes in v1:
time: 109 us
  Pallas kernels  103 us (94%)
  local copies, waits for them, and re-layouts  5.98 us (5%)
    pallas_call x1, Pallas kernels, shards(): pl.pallas_call(functools.partial(kernel, groups, ranks), out_shape=jax.Sh...  103 us
    unnamed x11, local copies, waits for them, and re-layouts  5.98 us

profile of v1, /device:TPU:0, one launch (start us, length us, event | category | flops | bytes accessed | tf_op | source)
XLA Modules:
  0.0 108.8 jit_solution(8522450162651090292)
XLA Ops:
  0.0 0.0 copy-start
  0.0 1.2 %copy-done = bf16[256,2048]{1,0:T(8,128)(2,1)S(1)} copy-done((bf16[256,2048]{1,0:T(8,128)(2,1)S(1)}, bf16[256,2048]{1,0:T(8,128)(2,1)}, u32[]{:S(2)}) %copy-start) | copy-done | bytes 1048600
  1.2 0.0 copy-start.1
  1.2 1.2 %copy-done.1 = bf16[256,2048]{1,0:T(8,128)(2,1)S(1)} copy-done((bf16[256,2048]{1,0:T(8,128)(2,1)S(1)}, bf16[256,2048]{1,0:T(8,128)(2,1)}, u32[]{:S(2)}) %copy-start.1) | copy-done | bytes 1048600
  2.5 0.0 copy-start.2
  2.5 1.2 %copy-done.2 = bf16[256,2048]{1,0:T(8,128)(2,1)S(1)} copy-done((bf16[256,2048]{1,0:T(8,128)(2,1)S(1)}, bf16[256,2048]{1,0:T(8,128)(2,1)}, u32[]{:S(2)}) %copy-start.2) | copy-done | bytes 1048600
  3.7 0.0 copy-start.3
  3.7 0.7 copy-done.3
  4.4 0.0 copy-start.4
  4.4 0.7 copy-done.4
  5.0 102.9 %shard_map.55 = bf16[256,2048]{1,0:T(8,128)(2,1)S(1)} custom-call(bf16[256,2048]{1,0:T(8,128)(2,1)S(1)} %copy-done, bf16[256,2048]{1,0:T(8,128)(2,1)S(1)} %copy-done.1, bf16[256,2048]{1,0:T(8,128)(2,1)S(1)} %copy-done.2, s32[2,8]{1,0:T(2,128)S(1)} %copy-done.3, s32[2]{0:T(128)S(1)} %copy-done.4), custom_call_target="tpu_custom_call" | custom-call | tf_op jit(solution)/shard_map/pallas_call | solution.py:178
  107.9 1.0 copy.7
Async XLA Ops:
  0.0 1.2 %copy-start = (bf16[256,2048]{1,0:T(8,128)(2,1)S(1)}, bf16[256,2048]{1,0:T(8,128)(2,1)}, u32[]{:S(2)}) copy-start(bf16[256,2048]{1,0:T(8,128)(2,1)} %q_hbm.1) | copy-start | bytes 3145732
  1.2 1.2 %copy-start.1 = (bf16[256,2048]{1,0:T(8,128)(2,1)S(1)}, bf16[256,2048]{1,0:T(8,128)(2,1)}, u32[]{:S(2)}) copy-start(bf16[256,2048]{1,0:T(8,128)(2,1)} %k_hbm.1) | copy-start | bytes 3145732
  2.5 1.2 %copy-start.2 = (bf16[256,2048]{1,0:T(8,128)(2,1)S(1)}, bf16[256,2048]{1,0:T(8,128)(2,1)}, u32[]{:S(2)}) copy-start(bf16[256,2048]{1,0:T(8,128)(2,1)} %v_hbm.1) | copy-start | bytes 3145732
  3.7 0.7 copy-start.3
  4.4 0.7 copy-start.4

commit v2 on v1

v2 whole, which is shorter than its diff:
```python
import functools
import math

import jax
import jax.numpy as jnp
from jax import lax
from jax.experimental import pallas as pl
from jax.experimental.pallas import tpu as pltpu
from jax.sharding import PartitionSpec as P

HD = 128
CHUNK_SIXTEENTHS = (4, 4, 4, 2, 1, 1)
MESH = pl.DeviceIdType.MESH


def kernel(
    groups,
    ranks,
    bounds,
    q_hbm,
    k_hbm,
    v_hbm,
    links_hbm,
    counts_hbm,
    o_ref,
    land,
    q_v,
    bias,
    send_sems,
    recv_sems,
    q_sem,
    links,
    counts,
    list_sems,
):
    _, slots, rows, _ = land.shape
    chunks = len(bounds) - 1
    tiles, lmax = links.shape
    tile_rows = rows // tiles
    g = lax.axis_index("group")
    r = lax.axis_index("rank")
    core = lax.rem(r, 2)
    partner = (g, r + 1 - 2 * core)
    upper = (2 * r) // ranks
    first = (g, lax.rem(r + ranks - 2 + 4 * upper, ranks))
    second = (g, lax.rem(r + ranks + 2 - 4 * upper, ranks))
    flows = [(first, 4 - 3 * upper), (second, 1 + 3 * upper)]
    crossed = groups == 4
    across = (g + 1 - 2 * lax.rem(g, 2), lax.rem(g + 2, 4))

    def peer_slot(source, at):
        return 4 + lax.rem(source - at + groups, groups)

    if crossed:
        for near in across:
            flows.append(((near, r), peer_slot(g, near)))
    else:
        for step in range(1, groups):
            flows.append(((lax.rem(g + groups - step, groups), r), 4 + step))
    flows.append((partner, 2 + core))
    relay = len(flows)
    hops = (across, across[::-1])

    barrier = pltpu.get_barrier_semaphore()
    for device, _ in flows:
        pl.semaphore_signal(barrier, inc=1, device_id=device, device_id_type=MESH)

    def columns(c):
        return pl.ds(bounds[c] * HD, (bounds[c + 1] - bounds[c]) * HD)

    def own_copy(c, kv):
        src = (k_hbm, v_hbm)[kv]
        return pltpu.make_async_copy(
            src.at[:, columns(c)], land.at[kv, 0, :, columns(c)], recv_sems.at[c, kv, 0]
        )

    def flow_copy(c, kv, f):
        device, slot = flows[f]
        src = (k_hbm, v_hbm)[kv]
        return pltpu.make_async_remote_copy(
            src_ref=src.at[:, columns(c)],
            dst_ref=land.at[kv, slot, :, columns(c)],
            send_sem=send_sems.at[c, kv, f],
            recv_sem=recv_sems.at[c, kv, slot],
            device_id=device,
            device_id_type=MESH,
        )

    def relay_copy(c, kv):
        return pltpu.make_async_remote_copy(
            src_ref=land.at[kv, 4 - 3 * core, :, columns(c)],
            dst_ref=land.at[kv, 3 - core, :, columns(c)],
            send_sem=send_sems.at[c, kv, relay],
            recv_sem=recv_sems.at[c, kv, 3 - core],
            device_id=partner,
            device_id_type=MESH,
        )

    def cross_copy(c, kv):
        source, target = hops[kv]
        slot = peer_slot(source, target)
        return pltpu.make_async_remote_copy(
            src_ref=land.at[kv, peer_slot(source, g), :, columns(c)],
            dst_ref=land.at[kv, slot, :, columns(c)],
            send_sem=send_sems.at[c, kv, relay + 1],
            recv_sem=recv_sems.at[c, kv, slot],
            device_id=(target, r),
            device_id_type=MESH,
        )

    def arrived(c, kv, slot):
        pltpu.make_async_remote_copy(
            src_ref=land.at[kv, slot, :, columns(c)],
            dst_ref=land.at[kv, slot, :, columns(c)],
            send_sem=send_sems.at[c, kv, 0],
            recv_sem=recv_sems.at[c, kv, slot],
            device_id=partner,
            device_id_type=MESH,
        ).wait_recv()

    def issue(c):
        for kv in range(2):
            for f in range(len(flows)):
                flow_copy(c, kv, f).start()

    local = [
        pltpu.make_async_copy(q_hbm, q_v, q_sem),
        pltpu.make_async_copy(links_hbm, links, list_sems.at[0]),
        pltpu.make_async_copy(counts_hbm, counts, list_sems.at[1]),
    ]
    for copy in local:
        copy.start()
    pl.semaphore_wait(barrier, len(flows))

    for c in range(chunks):
        issue(c)
    for c in range(chunks):
        for kv in range(2):
            own_copy(c, kv).start()

    for copy in local:
        copy.wait()
    cand = lax.broadcasted_iota(jnp.int32, (1, slots * rows), 1) // tile_rows
    for i in range(tiles):
        used = jnp.where(cand == i, 1, 0)
        for j in range(lmax):
            hit = jnp.where(j < counts[i], links[i, j], -1)
            used = used + jnp.where(cand == hit, 1, 0)
        bias[i, :, :] = jnp.where(used == 0, -jnp.inf, jnp.where(used == 2, 1.0, 0.0))

    scale = HD ** (-0.5) * math.log2(math.e)

    def attend(c):
        @pl.loop(bounds[c], bounds[c + 1])
        def _(h):
            head = pl.ds(pl.multiple_of(h * HD, HD), HD)
            keys = land[0, :, :, head].reshape(slots * rows, HD)
            values = land[1, :, :, head].reshape(slots * rows, HD)
            scores = lax.dot_general(
                q_v[:, head], keys, (((1,), (1,)), ((), ())), preferred_element_type=jnp.float32
            )
            scores = scores.reshape(tiles, tile_rows, slots * rows) * scale + bias[...]
            scores = scores.reshape(rows, slots * rows)
            weights = jnp.exp2(scores - jnp.max(scores, axis=1, keepdims=True))
            total = jnp.sum(weights, axis=1, keepdims=True)
            mixed = jnp.dot(
                weights.astype(jnp.bfloat16), values, preferred_element_type=jnp.float32
            )
            o_ref[:, head] = (mixed / total).astype(jnp.bfloat16)

    for c in range(chunks + 1):
        if c < chunks:
            for kv in range(2):
                arrived(c, kv, 4 - 3 * core)
                relay_copy(c, kv).start()
                if crossed:
                    arrived(c, kv, peer_slot(hops[kv][0], g))
                    cross_copy(c, kv).start()
        if c >= 1:
            b = c - 1
            for kv in range(2):
                own_copy(b, kv).wait()
                arrived(b, kv, 1 + 3 * core)
                for slot in (2, 3):
                    arrived(b, kv, slot)
                if crossed:
                    arrived(b, kv, peer_slot(hops[kv][1], g))
                    arrived(b, kv, peer_slot(3 - g, g))
                else:
                    for slot in range(5, slots):
                        arrived(b, kv, slot)
            attend(b)

    for c in range(chunks):
        for kv in range(2):
            for f in range(len(flows)):
                flow_copy(c, kv, f).wait_send()
            relay_copy(c, kv).wait_send()
            if crossed:
                cross_copy(c, kv).wait_send()


def shards(groups, ranks, queries, key_rows, value_rows, tile_links, link_counts):
    rows, features = queries.shape
    tiles = tile_links.shape[0]
    slots = 4 + groups
    heads = features // HD
    bounds = [0]
    for part in CHUNK_SIXTEENTHS:
        bounds.append(bounds[-1] + part * heads // 16)
    chunks = len(bounds) - 1
    hbm = pl.BlockSpec(memory_space=pl.ANY)
    return pl.pallas_call(
        functools.partial(kernel, groups, ranks, tuple(bounds)),
        out_shape=jax.ShapeDtypeStruct((rows, features), jnp.bfloat16),
        in_specs=[hbm] * 5,
        out_specs=pl.BlockSpec(memory_space=pltpu.VMEM),
        scratch_shapes=[
            pltpu.VMEM((2, slots, rows, features), jnp.bfloat16),
            pltpu.VMEM((rows, features), jnp.bfloat16),
            pltpu.VMEM((tiles, 1, slots * rows), jnp.float32),
            pltpu.SemaphoreType.DMA((chunks, 2, groups + 4)),
            pltpu.SemaphoreType.DMA((chunks, 2, slots + 1)),
            pltpu.SemaphoreType.DMA,
            pltpu.SMEM(tile_links.shape, jnp.int32),
            pltpu.SMEM(link_counts.shape, jnp.int32),
            pltpu.SemaphoreType.DMA((2,)),
        ],
        compiler_params=pltpu.CompilerParams(
            collective_id=0, has_side_effects=True, vmem_limit_bytes=62 * 2**20
        ),
    )(queries, key_rows, value_rows, tile_links, link_counts)


def solution(mesh):
    nodes = P(("group", "rank"), None)
    return jax.shard_map(
        functools.partial(shards, mesh.shape["group"], mesh.shape["rank"]),
        mesh=mesh,
        in_specs=(nodes, nodes, nodes, nodes, P(("group", "rank"))),
        out_specs=nodes,
        check_vma=False,
    )
```

time: 109 us -> 104 us (0.954)
  local copies, waits for them, and re-layouts: 5.98 us -> 2.3 us
  Pallas kernels: 103 us -> 101 us
    unnamed x11 -> x1, local copies, waits for them, and re-layouts: 5.98 us -> 2.3 us
    pallas_call x1, Pallas kernels: 103 us -> 101 us  [shards(): pl.pallas_call(functools.partial(kernel, groups, ranks, tuple(bounds)), o...]
where the time goes in v2:
time: 104 us; the launch traced here: 103 us
  Pallas kernels  101 us (97%)
  local copies, waits for them, and re-layouts  2.3 us (2%)
    pallas_call x1, Pallas kernels, shards(): pl.pallas_call(functools.partial(kernel, groups, ranks, tuple(bounds)), o...  101 us
    unnamed x1, local copies, waits for them, and re-layouts  2.3 us

profile of v2, /device:TPU:0, one launch (start us, length us, event | category | flops | bytes accessed | tf_op | source)
XLA Modules:
  0.0 103.4 jit_solution(16439287738624565986)
XLA Ops:
  0.0 101.0 %shard_map.55 = bf16[256,2048]{1,0:T(8,128)(2,1)} custom-call(bf16[256,2048]{1,0:T(8,128)(2,1)} %q_hbm.1, bf16[256,2048]{1,0:T(8,128)(2,1)} %k_hbm.1, bf16[256,2048]{1,0:T(8,128)(2,1)} %v_hbm.1, s32[2,8]{1,0:T(2,128)} %links_hbm.1, s32[2]{0:T(128)} %counts_hbm.1), custom_call_target="tpu_custom_call" | custom-call | tf_op jit(solution)/shard_map/pallas_call | solution.py:213
  101.0 2.3 %copy.7 = bf16[256,2048]{1,0:T(8,128)(2,1)} copy(bf16[256,2048]{1,0:T(8,128)(2,1)} %shard_map.55) | data formatting | bytes 2097152
